TPU v7x, 128 devices: a whole 4x4x4 slice. The times are simulated.
128 devices in a mesh: rows: 16 (over z, y), cols: 8 (over x, core).
Axes of the slice: x: 4, y: 4, z: 4, core: 2. Of those that a mesh axis runs over, the one named last changes fastest.
Arguments:
- grad_stack: float32 [512, 64, 2048], P(None, 'rows', 'cols'), may hold values from -6 to 6
- moment_stack: float32 [512, 64, 2048], P(None, 'rows', 'cols'), may hold values from -6 to 6
- weight_stack: float32 [512, 64, 2048], P(None, 'rows', 'cols'), may hold values from -0.1875 to 0.1875
Outputs:
- new_weights: float32 [512, 64, 2048], P(None, 'rows', 'cols')
- new_momentum: float32 [512, 64, 2048], P(None, 'rows', 'cols')
All inputs are finite; a program needn't handle non-finite values.
Results may differ from a plain program's by a relative error of at most 0.0003.
Values sent between devices are 32-bit elements.
A program may use at most 128 MiB of HBM per device.

v0:
```python
import functools

import jax
import jax.numpy as jnp
from jax import lax
from jax.experimental import pallas as pl
from jax.experimental.pallas import tpu as pltpu
from jax.sharding import PartitionSpec as P

ITERS = 5
CHUNKS = 4

hold_rate = 0.95
learn_rate = 1.0

MESH = pl.DeviceIdType.MESH


def mul(a, b):
    return lax.dot_general(
        a, b, (((1,), (0,)), ((), ())),
        precision=lax.Precision.HIGHEST, preferred_element_type=jnp.float32,
    )


def mul_t(a, b):
    return lax.dot_general(
        a, b, (((1,), (1,)), ((), ())),
        precision=lax.Precision.HIGHEST, preferred_element_type=jnp.float32,
    )


def transform(packed, side):
    wide = 2 * side
    row = lax.broadcasted_iota(jnp.int32, (side, wide), 0)
    lane = lax.broadcasted_iota(jnp.int32, (side, wide), 1)
    first = lane < side
    scales = [
        lax.rsqrt(
            jnp.sum(
                jnp.sum(jnp.where(lane == row + at, packed, 0.0), axis=1, keepdims=True),
                axis=0, keepdims=True,
            ) + 1e-06
        )
        for at in (0, side)
    ]
    scale = jnp.where(first, scales[0], scales[1])
    scaled = packed * scale * scale
    gram = jnp.concatenate(
        [jnp.where(first, scaled, 0.0), jnp.where(first, 0.0, scaled)], axis=0
    )
    eye = lax.broadcasted_iota(jnp.int32, (wide, wide), 0) == lax.broadcasted_iota(
        jnp.int32, (wide, wide), 1
    )
    total = None
    for step in range(ITERS):
        factor = jnp.where(eye, 3.4445, 0.0) + (-4.775 * gram + 2.0315 * mul(gram, gram))
        total = factor if total is None else mul(factor, total)
        if step < ITERS - 1:
            gram = mul(factor, mul(factor, gram))
    return total * jnp.concatenate([scale, scale], axis=0)


def kernel(
    rows, cols, chunks, mom, back, held, made, mine, theirs, total, pair_buf,
    out_send, out_recv, gram_send, gram_recv, ret_send, ret_recv, own_sem,
):
    me, col = lax.axis_index("rows"), lax.axis_index("cols")
    _, mats, share, width = held.shape
    side = rows * share
    count = mats // chunks
    pairs = count // 2

    def row_peer(k):
        return lax.rem(me + k, rows)

    def col_peer(k):
        return lax.rem(col + k, cols)

    barrier = pltpu.get_barrier_semaphore()
    for k in range(1, rows):
        pl.semaphore_signal(barrier, inc=1, device_id=(row_peer(k), col), device_id_type=MESH)
    for k in range(1, cols):
        pl.semaphore_signal(barrier, inc=1, device_id=(me, col_peer(k)), device_id_type=MESH)
    pl.semaphore_wait(barrier, rows + cols - 2)

    def outgoing(c, k):
        to = row_peer(k)
        return pltpu.make_async_remote_copy(
            src_ref=mom.at[pl.ds(to * mats + c * count, count)],
            dst_ref=held.at[me, pl.ds(c * count, count)],
            send_sem=out_send.at[c, k - 1],
            recv_sem=out_recv.at[c, k - 1],
            device_id=(to, col),
            device_id_type=MESH,
        )

    def grams(c, k):
        return pltpu.make_async_remote_copy(
            src_ref=mine.at[pl.ds(c * pairs, pairs)],
            dst_ref=theirs.at[k - 1, pl.ds(c * pairs, pairs)],
            send_sem=gram_send.at[c, k - 1],
            recv_sem=gram_recv.at[c, k - 1],
            device_id=(me, col_peer(k)),
            device_id_type=MESH,
        )

    def returning(c, k):
        to = row_peer(k)
        return pltpu.make_async_remote_copy(
            src_ref=made.at[to, pl.ds(c * count, count)],
            dst_ref=back.at[pl.ds(me * mats + c * count, count)],
            send_sem=ret_send.at[c, k - 1],
            recv_sem=ret_recv.at[c, k - 1],
            device_id=(to, col),
            device_id_type=MESH,
        )

    def own_back(c):
        return pltpu.make_async_copy(
            made.at[me, pl.ds(c * count, count)],
            back.at[pl.ds(me * mats + c * count, count)],
            own_sem.at[c + 1],
        )

    own_in = pltpu.make_async_copy(mom.at[pl.ds(me * mats, mats)], held.at[me], own_sem.at[0])

    @pl.loop(0, chunks)
    def _(c):
        for k in range(1, rows):
            outgoing(c, k).start()

    own_in.start()
    own_in.wait()

    def load_pair(m):
        if share % 8 == 0:
            return jnp.concatenate(
                [held[:, m + at].reshape(side, width) for at in (0, 1)], axis=0
            )
        for at in (0, 1):
            for s in range(rows):
                pair_buf[pl.ds(at * side + s * share, share), :] = held[s, m + at]
        return pair_buf[...]

    def store_pair(m, value):
        if share % 8 == 0:
            for at in (0, 1):
                made[:, m + at] = value[at * side:(at + 1) * side].reshape(rows, share, width)
            return
        pair_buf[...] = value
        for at in (0, 1):
            for s in range(rows):
                made[s, m + at] = pair_buf[pl.ds(at * side + s * share, share), :]

    @pl.loop(0, chunks)
    def _(c):
        for k in range(1, rows):
            outgoing(c, k).wait_recv()

        @pl.loop(0, pairs)
        def _(p):
            x = load_pair(c * count + 2 * p)
            both = mul_t(x, x)
            lane = lax.broadcasted_iota(jnp.int32, (side, 2 * side), 1)
            mine[c * pairs + p] = jnp.where(lane < side, both[:side], both[side:])

        for k in range(1, cols):
            grams(c, k).start()
        for k in range(1, cols):
            grams(c, k).wait_recv()

        packed = []
        for p in range(pairs):
            at = c * pairs + p
            one = mine[at]
            for k in range(1, cols):
                one = one + theirs[k - 1, at]
            packed.append(one)
        for p, one in enumerate(packed):
            total[p] = transform(one, side)

        @pl.loop(0, pairs)
        def _(p):
            m = c * count + 2 * p
            store_pair(m, mul(total[p], load_pair(m)))

        for k in range(1, rows):
            returning(c, k).start()
        own_back(c).start()

    @pl.loop(0, chunks)
    def _(c):
        for k in range(1, rows):
            returning(c, k).wait_recv()
            returning(c, k).wait_send()
            outgoing(c, k).wait_send()
        for k in range(1, cols):
            grams(c, k).wait_send()
        own_back(c).wait()


def exchange_and_iterate(new_momentum, rows, cols):
    every, share, width = new_momentum.shape
    mats = every // rows
    side = rows * share
    chunks = CHUNKS
    pairs = mats // chunks // 2
    f32, dma = jnp.float32, pltpu.SemaphoreType.DMA
    return pl.pallas_call(
        functools.partial(kernel, rows, cols, chunks),
        out_shape=jax.ShapeDtypeStruct((every, share, width), f32),
        in_specs=[pl.BlockSpec(memory_space=pl.ANY)],
        out_specs=pl.BlockSpec(memory_space=pl.ANY),
        scratch_shapes=[
            pltpu.VMEM((rows, mats, share, width), f32),
            pltpu.VMEM((rows, mats, share, width), f32),
            pltpu.VMEM((mats // 2, side, 2 * side), f32),
            pltpu.VMEM((cols - 1, mats // 2, side, 2 * side), f32),
            pltpu.VMEM((pairs, 2 * side, 2 * side), f32),
            pltpu.VMEM((2 * side, width), f32),
            dma((chunks, rows - 1)),
            dma((chunks, rows - 1)),
            dma((chunks, cols - 1)),
            dma((chunks, cols - 1)),
            dma((chunks, rows - 1)),
            dma((chunks, rows - 1)),
            dma((chunks + 1,)),
        ],
        compiler_params=pltpu.CompilerParams(
            collective_id=0, has_side_effects=True, vmem_limit_bytes=48 * 2**20
        ),
        name="exchange_and_iterate",
    )(new_momentum)


def solution(mesh):
    rows, cols = mesh.shape["rows"], mesh.shape["cols"]

    def on_device(grad_stack, moment_stack, weight_stack):
        new_momentum = hold_rate * moment_stack + grad_stack
        back = exchange_and_iterate(new_momentum, rows, cols)
        new_weights = weight_stack - learn_rate * back
        return (new_weights, new_momentum)

    placed = P(None, "rows", "cols")
    return jax.shard_map(
        on_device,
        mesh=mesh,
        in_specs=(placed, placed, placed),
        out_specs=(placed, placed),
        check_vma=False,
    )
```

profile of v0, /device:TPU:0, one launch (start us, length us, event | category | flops | bytes accessed | tf_op | source)
XLA Modules:
  0.0 139.9 jit_solution(8925340363711698809)
XLA Ops:
  0.6 2.9 %multiply_add_fusion.mom = f32[512,4,256]{2,1,0:T(4,128)S(1)} fusion(f32[512,4,256]{2,1,0:T(4,128)} %param.3, f32[512,4,256]{2,1,0:T(4,128)} %param.4), kind=kLoop, calls=%fused_computation | loop fusion | flops 1048576 | bytes 6291456 | tf_op jit(solution)/shard_map/add | solution.py:241
  3.6 0.0 copy-start
  3.6 0.0 copy-start.1
  3.6 134.4 %exchange_and_iterate.1 = f32[512,4,256]{2,1,0:T(4,128)S(1)} custom-call(f32[512,4,256]{2,1,0:T(4,128)S(1)} %multiply_add_fusion.mom), custom_call_target="tpu_custom_call" | custom-call | tf_op jit(solution)/shard_map/exchange_and_iterate/pallas_call | solution.py:210
  138.0 0.0 copy-done.1
  138.1 1.9 %sub.3 = f32[512,4,256]{2,1,0:T(4,128)} subtract(f32[512,4,256]{2,1,0:T(4,128)S(1)} %copy-done.1, f32[512,4,256]{2,1,0:T(4,128)S(1)} %exchange_and_iterate.1) | non-fusion elementwise | flops 524288 | bytes 6291456 | tf_op jit(solution)/shard_map/sub | solution.py:243
  139.9 0.0 copy-done
Async XLA Ops:
  3.6 136.3 %copy-start = (f32[512,4,256]{2,1,0:T(4,128)}, f32[512,4,256]{2,1,0:T(4,128)S(1)}, u32[]{:S(2)}) copy-start(f32[512,4,256]{2,1,0:T(4,128)S(1)} %multiply_add_fusion.mom) | copy-start | bytes 6291460
  3.6 134.5 %copy-start.1 = (f32[512,4,256]{2,1,0:T(4,128)S(1)}, f32[512,4,256]{2,1,0:T(4,128)}, u32[]{:S(2)}) copy-start(f32[512,4,256]{2,1,0:T(4,128)} %param.5) | copy-start | bytes 6291460
where the time goes:
time: 142 us; the launch traced here: 140 us
  Pallas kernels  134 us (94%)
  other arithmetic  4.8 us (3%)
    pallas_call x1, Pallas kernels, exchange_and_iterate(): pl.pallas_call(functools.partial(kernel, rows, cols, chunks), out_shape=j...  134 us
    add x1, other arithmetic, on_device(): new_momentum = hold_rate * moment_stack + grad_stack  2.94 us

commit v1 on v0

v1 whole, which is shorter than its diff:
```python
import functools

import jax
import jax.numpy as jnp
from jax import lax
from jax.experimental import pallas as pl
from jax.experimental.pallas import tpu as pltpu
from jax.sharding import PartitionSpec as P

ITERS = 5
RING = 4
CHUNKS = 4
AHEAD = 2

hold_rate = 0.95
learn_rate = 1.0

MESH = pl.DeviceIdType.MESH


def mul(a, b):
    return lax.dot_general(
        a, b, (((1,), (0,)), ((), ())),
        precision=lax.Precision.HIGHEST, preferred_element_type=jnp.float32,
    )


def mul_t(a, b):
    return lax.dot_general(
        a, b, (((1,), (1,)), ((), ())),
        precision=lax.Precision.HIGHEST, preferred_element_type=jnp.float32,
    )


def spread(packed, side):
    first = lax.broadcasted_iota(jnp.int32, (side, 2 * side), 1) < side
    return jnp.concatenate(
        [jnp.where(first, packed, 0.0), jnp.where(first, 0.0, packed)], axis=0
    )


def transform(packed, side):
    wide = 2 * side
    row = lax.broadcasted_iota(jnp.int32, (side, wide), 0)
    lane = lax.broadcasted_iota(jnp.int32, (side, wide), 1)
    first = lane < side
    scales = [
        lax.rsqrt(
            jnp.sum(
                jnp.sum(jnp.where(lane == row + at, packed, 0.0), axis=1, keepdims=True),
                axis=0, keepdims=True,
            ) + 1e-06
        )
        for at in (0, side)
    ]
    scale = jnp.where(first, scales[0], scales[1])
    gram = spread(packed * scale * scale, side)
    eye = lax.broadcasted_iota(jnp.int32, (wide, wide), 0) == lax.broadcasted_iota(
        jnp.int32, (wide, wide), 1
    )
    total = None
    for step in range(ITERS):
        factor = jnp.where(eye, 3.4445, 0.0) + (-4.775 * gram + 2.0315 * mul(gram, gram))
        total = factor if total is None else mul(factor, total)
        if step < ITERS - 1:
            gram = mul(factor, mul(factor, gram))
    return jnp.where(first, total[:side], total[side:]) * scale


def kernel(
    cols, mom, back, mid, held, made, omid, xs, obuf, mine, theirs, fac,
    in1_s, in1_r, in2_s, in2_r, in3_s, in3_r, rs_s, rs_r, ag_s, ag_r,
    o1_s, o1_r, o2_s, o2_r, o3_s, o3_r, own_sem,
):
    me, col = lax.axis_index("rows"), lax.axis_index("cols")
    z, y = me // RING, lax.rem(me, RING)
    place, core = col // 2, lax.rem(col, 2)
    mats, share, width = mom.shape[2:]
    side = RING * RING * share
    count = mats // CHUNKS
    half = count // 2
    pairs = count // 2
    others = range(1, RING)
    order = (1, 3, 2)

    def up(at, k):
        return lax.rem(at + k, RING)

    def down(at, k):
        return lax.rem(at + RING - k, RING)

    def along(h, at):
        return (z * RING + at, col) if h == 0 else (at * RING + y, col)

    def col_peer(k):
        return lax.rem(col + k, cols)

    barrier = pltpu.get_barrier_semaphore()
    for k in others:
        for h in (0, 1):
            pl.semaphore_signal(
                barrier, inc=1, device_id=along(h, up((y, z)[h], k)), device_id_type=MESH
            )
    for k in range(1, cols):
        pl.semaphore_signal(barrier, inc=1, device_id=(me, col_peer(k)), device_id_type=MESH)
    pl.semaphore_wait(barrier, 2 * (RING - 1) + cols - 1)

    def remote(src, dst, send, recv, to):
        return pltpu.make_async_remote_copy(
            src_ref=src, dst_ref=dst, send_sem=send, recv_sem=recv,
            device_id=to, device_id_type=MESH,
        )

    def of(h, c):
        return pl.ds(c * count + h * half, half), pl.ds(c * half, half)

    def in1(c, h, k):
        at, near = of(h, c)
        to = up((y, z)[h], k)
        src = mom.at[:, to, at] if h == 0 else mom.at[to, :, at]
        return remote(src, mid.at[h, k, :, near], in1_s.at[c, h, k], in1_r.at[c, h, k], along(h, to))

    def in2(c, h, k):
        at, near = of(h, c)
        to = up((z, y)[h], k)
        dst = held.at[k, pl.ds(1, RING - 1), at] if h == 0 else held.at[pl.ds(1, RING - 1), k, at]
        return remote(
            mid.at[h, pl.ds(1, RING - 1), to, near], dst,
            in2_s.at[c, h, k], in2_r.at[c, h, k], along(1 - h, to),
        )

    def in3(c, h, k):
        at, _ = of(h, c)
        to = up((z, y)[h], k)
        src, dst = (
            (mom.at[to, y, at], held.at[k, 0, at]) if h == 0
            else (mom.at[z, to, at], held.at[0, k, at])
        )
        return remote(src, dst, in3_s.at[c, h, k], in3_r.at[c, h, k], along(1 - h, to))

    def out1(c, h, k):
        at, near = of(h, c)
        to = down((z, y)[h], k)
        src, dst = (
            (made.at[k, pl.ds(1, RING - 1), at], omid.at[0, pl.ds(1, RING - 1), z, near]) if h == 0
            else (made.at[pl.ds(1, RING - 1), k, at], omid.at[1, pl.ds(1, RING - 1), y, near])
        )
        return remote(src, dst, o1_s.at[c, h, k], o1_r.at[c, h, k], along(1 - h, to))

    def out3(c, h, k):
        at, _ = of(h, c)
        to = down((z, y)[h], k)
        src = made.at[k, 0, at] if h == 0 else made.at[0, k, at]
        return remote(
            src, back.at[z, y, at], o3_s.at[c, h, k], o3_r.at[c, h, k], along(1 - h, to)
        )

    def out2(c, h, k):
        at, near = of(h, c)
        to = down((y, z)[h], k)
        dst = back.at[:, y, at] if h == 0 else back.at[z, :, at]
        return remote(
            omid.at[h, k, :, near], dst, o2_s.at[c, h, k], o2_r.at[c, h, k], along(h, to)
        )

    def own_back(c):
        at = pl.ds(c * count, count)
        return pltpu.make_async_copy(made.at[0, 0, at], back.at[z, y, at], own_sem.at[c + 1])

    def worker(c, p):
        return 2 * p + lax.rem(c, 2)

    def gram_send(c, p):
        to = worker(c, p)
        k = lax.rem(col + cols - to, cols)
        return remote(
            mine.at[c, p], theirs.at[c, k], rs_s.at[c, p], rs_r.at[c, k], (me, to)
        )

    def gram_recv(c, k):
        return remote(
            mine.at[c, 0], theirs.at[c, k], rs_s.at[c, 0], rs_r.at[c, k], (me, col_peer(k))
        )

    def fac_copy(c, p, k):
        return remote(
            fac.at[c, p], fac.at[c, p], ag_s.at[c, k], ag_r.at[c, p], (me, col_peer(k))
        )

    own_in = pltpu.make_async_copy(mom.at[z, y], held.at[0, 0], own_sem.at[0])
    own_in.start()

    def start_in1(c):
        for k in order:
            for h in (0, 1):
                in1(c, h, k).start()

    for c in range(AHEAD):
        start_in1(c)
    own_in.wait()

    def rows_of(h, i, m, near):
        dz, dy = i // RING, i % RING
        if h == 0 and dz == 0 and dy > 0:
            return mid[0, dy, z, near]
        if h == 1 and dy == 0 and dz > 0:
            return mid[1, dz, y, near]
        return held[dz, dy, m]

    def keep_rows(h, i, m, near, value):
        dz, dy = i // RING, i % RING
        if h == 0 and dz == 0 and dy > 0:
            omid[0, dy, z, near] = value
        elif h == 1 and dy == 0 and dz > 0:
            omid[1, dz, y, near] = value
        else:
            made[dz, dy, m] = value

    def gram_stage(c):
        for k in others:
            for h in (0, 1):
                in2(c, h, k).wait_recv()
                in3(c, h, k).wait_recv()
        first = lax.broadcasted_iota(jnp.int32, (side, 2 * side), 1) < side

        @pl.loop(0, pairs // 2)
        def _(q):
            for h in (0, 1):
                p = h * (pairs // 2) + q
                for at in (0, 1):
                    near = c * half + 2 * q + at
                    m = c * count + h * half + 2 * q + at
                    for i in range(RING * RING):
                        xs[c, p, pl.ds(at * side + i * share, share), :] = rows_of(h, i, m, near)
            for h in (0, 1):
                p = h * (pairs // 2) + q
                x = xs[c, p]
                both = mul_t(x, x)
                mine[c, p] = jnp.where(first, both[:side], both[side:])

        for p in range(pairs):
            @pl.when(worker(c, p) != col)
            def _():
                gram_send(c, p).start()

    def transform_stage(c):
        @pl.when(core == lax.rem(c, 2))
        def _():
            for k in range(1, cols):
                gram_recv(c, k).wait_recv()
            one = mine[c, place]
            for k in range(1, cols):
                one = one + theirs[c, k]
            fac[c, place] = transform(one, side)
            for k in range(1, cols):
                fac_copy(c, place, k).start()

    def apply_stage(c):
        for p in range(pairs):
            @pl.when(worker(c, p) != col)
            def _():
                fac_copy(c, p, 1).wait_recv()

        @pl.loop(0, pairs // 2)
        def _(q):
            for h in (0, 1):
                p = h * (pairs // 2) + q
                obuf[h] = mul(spread(fac[c, p], side), xs[c, p])
            for h in (0, 1):
                for at in (0, 1):
                    near = c * half + 2 * q + at
                    m = c * count + h * half + 2 * q + at
                    for i in range(RING * RING):
                        keep_rows(h, i, m, near, obuf[h, pl.ds(at * side + i * share, share), :])

        for k in order:
            for h in (0, 1):
                out1(c, h, k).start()
                out3(c, h, k).start()
        own_back(c).start()

    @pl.loop(0, CHUNKS + 4)
    def _(t):
        @pl.when(t < CHUNKS)
        def _():
            for k in order:
                for h in (0, 1):
                    in1(t, h, k).wait_recv()
            for k in order:
                for h in (0, 1):
                    in2(t, h, k).start()
                    in3(t, h, k).start()

        @pl.when(t + AHEAD < CHUNKS)
        def _():
            start_in1(t + AHEAD)

        @pl.when(t >= 4)
        def _():
            c = t - 4
            for k in order:
                for h in (0, 1):
                    out1(c, h, k).wait_recv()
            for k in order:
                for h in (0, 1):
                    out2(c, h, k).start()

        @pl.when((t >= 1) & (t < CHUNKS + 1))
        def _():
            gram_stage(t - 1)

        @pl.when((t >= 2) & (t < CHUNKS + 2))
        def _():
            transform_stage(t - 2)

        @pl.when((t >= 3) & (t < CHUNKS + 3))
        def _():
            apply_stage(t - 3)

    @pl.loop(0, CHUNKS)
    def _(c):
        for k in others:
            for h in (0, 1):
                in1(c, h, k).wait_send()
                in2(c, h, k).wait_send()
                in3(c, h, k).wait_send()
                out1(c, h, k).wait_send()
                out2(c, h, k).wait()
                out3(c, h, k).wait()
        for p in range(pairs):
            @pl.when(worker(c, p) != col)
            def _():
                gram_send(c, p).wait_send()

        @pl.when(core == lax.rem(c, 2))
        def _():
            for k in range(1, cols):
                fac_copy(c, place, k).wait_send()
        own_back(c).wait()


def exchange_and_iterate(new_momentum, cols):
    every, share, width = new_momentum.shape
    mats = every // (RING * RING)
    side = RING * RING * share
    count = mats // CHUNKS
    pairs = count // 2
    f32, dma = jnp.float32, pltpu.SemaphoreType.DMA
    hops = dma((CHUNKS, 2, RING))
    shape = (RING, RING, mats, share, width)
    out = pl.pallas_call(
        functools.partial(kernel, cols),
        out_shape=jax.ShapeDtypeStruct(shape, f32),
        in_specs=[pl.BlockSpec(memory_space=pl.ANY)],
        out_specs=pl.BlockSpec(memory_space=pl.ANY),
        scratch_shapes=[
            pltpu.VMEM((2, RING, RING, mats // 2, share, width), f32),
            pltpu.VMEM(shape, f32),
            pltpu.VMEM(shape, f32),
            pltpu.VMEM((2, RING, RING, mats // 2, share, width), f32),
            pltpu.VMEM((CHUNKS, pairs, 2 * side, width), f32),
            pltpu.VMEM((2, 2 * side, width), f32),
            pltpu.VMEM((CHUNKS, pairs, side, 2 * side), f32),
            pltpu.VMEM((CHUNKS, cols, side, 2 * side), f32),
            pltpu.VMEM((CHUNKS, pairs, side, 2 * side), f32),
            hops, hops, hops, hops, hops, hops,
            dma((CHUNKS, pairs)), dma((CHUNKS, cols)),
            dma((CHUNKS, cols)), dma((CHUNKS, pairs)),
            hops, hops, hops, hops, hops, hops,
            dma((CHUNKS + 1,)),
        ],
        compiler_params=pltpu.CompilerParams(
            collective_id=0, has_side_effects=True, vmem_limit_bytes=40 * 2**20
        ),
        name="exchange_and_iterate",
    )(new_momentum.reshape(shape))
    return out.reshape(every, share, width)


def solution(mesh):
    cols = mesh.shape["cols"]

    def on_device(grad_stack, moment_stack, weight_stack):
        new_momentum = hold_rate * moment_stack + grad_stack
        back = exchange_and_iterate(new_momentum, cols)
        new_weights = weight_stack - learn_rate * back
        return (new_weights, new_momentum)

    placed = P(None, "rows", "cols")
    return jax.shard_map(
        on_device,
        mesh=mesh,
        in_specs=(placed, placed, placed),
        out_specs=(placed, placed),
        check_vma=False,
    )
```

time: 142 us -> 78.1 us (0.55); the launches traced: 140 us -> 78 us
  Pallas kernels: 134 us -> 72.4 us
    pallas_call x1, Pallas kernels: 134 us -> 72.4 us  [exchange_and_iterate(): pl.pallas_call(functools.partial(kernel, cols), out_shape=jax.ShapeDtypeS...]
where the time goes in v1:
time: 78.1 us; the launch traced here: 78 us
  Pallas kernels  72.4 us (93%)
  other arithmetic  4.94 us (6%)
    pallas_call x1, Pallas kernels, exchange_and_iterate(): pl.pallas_call(functools.partial(kernel, cols), out_shape=jax.ShapeDtypeS...  72.4 us
    add x1, other arithmetic, on_device(): new_momentum = hold_rate * moment_stack + grad_stack  2.94 us
    sub x1, other arithmetic, on_device(): new_weights = weight_stack - learn_rate * back  2 us

profile of v1, /device:TPU:0, one launch (start us, length us, event | category | flops | bytes accessed | tf_op | source)
XLA Modules:
  0.0 78.0 jit_solution(1972699311461726559)
XLA Ops:
  0.6 2.9 %multiply_add_fusion = f32[512,4,256]{2,1,0:T(4,128)S(1)} fusion(f32[512,4,256]{2,1,0:T(4,128)} %param.3, f32[512,4,256]{2,1,0:T(4,128)} %param.4), kind=kLoop, calls=%fused_computation.1 | loop fusion | flops 1048576 | bytes 6291456 | tf_op jit(solution)/shard_map/add | solution.py:384
  3.6 0.0 copy-start
  3.6 0.0 copy-start.1
  3.6 72.4 %exchange_and_iterate.1 = f32[4,4,32,4,256]{4,3,2,1,0:T(4,128)S(1)} custom-call(f32[4,4,32,4,256]{4,3,2,1,0:T(4,128)S(1)} %bitcast.3), custom_call_target="tpu_custom_call" | custom-call | tf_op jit(solution)/shard_map/exchange_and_iterate/pallas_call | solution.py:351
  76.0 0.0 copy-done
  76.0 0.0 copy-done.1
  76.0 2.0 %bitcast_subtract_fusion = f32[512,4,256]{2,1,0:T(4,128)} fusion(f32[512,4,256]{2,1,0:T(4,128)S(1)} %copy-done.1, f32[4,4,32,4,256]{4,3,2,1,0:T(4,128)S(1)} %exchange_and_iterate.1), kind=kLoop, calls=%fused_computation | loop fusion | flops 524288 | bytes 6291456 | tf_op jit(solution)/shard_map/sub | solution.py:386
Async XLA Ops:
  3.6 72.4 %copy-start = (f32[512,4,256]{2,1,0:T(4,128)}, f32[512,4,256]{2,1,0:T(4,128)S(1)}, u32[]{:S(2)}) copy-start(f32[512,4,256]{2,1,0:T(4,128)S(1)} %multiply_add_fusion) | copy-start | bytes 6291460
  3.6 72.4 %copy-start.1 = (f32[512,4,256]{2,1,0:T(4,128)S(1)}, f32[512,4,256]{2,1,0:T(4,128)}, u32[]{:S(2)}) copy-start(f32[512,4,256]{2,1,0:T(4,128)} %param.5) | copy-start | bytes 6291460

commit v2 on v1

v2 whole, which is shorter than its diff:
```python
import functools

import jax
import jax.numpy as jnp
from jax import lax
from jax.experimental import pallas as pl
from jax.experimental.pallas import tpu as pltpu
from jax.sharding import PartitionSpec as P

ITERS = 5
RING = 4
CHUNKS = 8
OUT_HOPS = 2
SCHEDULE = (
    "M0", "M4", "B0", "S4", "M2", "M1", "M5", "M3", "S3", "S1", "S2", "I4", "I3", "I1",
    "I2", "S5", "S0", "G4", "G3", "M6", "M7", "S6", "S7", "G1", "G2", "I5", "T4", "I0",
    "T3", "I6", "T1", "I7", "T2", "A4", "G5", "A3", "G0", "G6", "A1", "G7", "A2", "O4",
    "T5", "O3", "T6", "T0", "O1", "T7", "O2", "A5", "A0", "A6", "A7", "O5", "O0", "O6",
    "O7",
)

hold_rate = 0.95
learn_rate = 1.0

MESH = pl.DeviceIdType.MESH


def mul(a, b):
    return lax.dot_general(
        a, b, (((1,), (0,)), ((), ())),
        precision=lax.Precision.HIGHEST, preferred_element_type=jnp.float32,
    )


def mul_t(a, b):
    return lax.dot_general(
        a, b, (((1,), (1,)), ((), ())),
        precision=lax.Precision.HIGHEST, preferred_element_type=jnp.float32,
    )


def spread(packed, side):
    first = lax.broadcasted_iota(jnp.int32, (side, 2 * side), 1) < side
    return jnp.concatenate(
        [jnp.where(first, packed, 0.0), jnp.where(first, 0.0, packed)], axis=0
    )


def parts(x):
    high = x.astype(jnp.bfloat16)
    rest = x - high.astype(jnp.float32)
    mid = rest.astype(jnp.bfloat16)
    low = (rest - mid.astype(jnp.float32)).astype(jnp.bfloat16)
    return high, mid, low


def right(x, side):
    high, mid, low = (part.astype(jnp.bfloat16) for part in map(
        lambda part: spread(part.astype(jnp.float32), side), parts(x)
    ))
    both = jnp.concatenate(
        [jnp.concatenate([high, mid], axis=1), jnp.concatenate([mid, high], axis=1)], axis=0
    )
    return both, jnp.concatenate([low, high], axis=0)


def times(x, factors):
    both, rest = factors
    wide = rest.shape[1]
    high, mid, low = parts(x)

    def dot(a, b):
        return jnp.dot(a, b, preferred_element_type=jnp.float32)

    large = dot(jnp.concatenate([high, mid], axis=1), both)
    small = dot(jnp.concatenate([high, low], axis=1), rest)
    return large[:, :wide] + (large[:, wide:] + small)


def transform(packed, side):
    wide = 2 * side
    row = lax.broadcasted_iota(jnp.int32, (side, wide), 0)
    lane = lax.broadcasted_iota(jnp.int32, (side, wide), 1)
    first = lane < side
    scales = [
        lax.rsqrt(
            jnp.sum(
                jnp.sum(jnp.where(lane == row + at, packed, 0.0), axis=1, keepdims=True),
                axis=0, keepdims=True,
            ) + 1e-06
        )
        for at in (0, side)
    ]
    scale = jnp.where(first, scales[0], scales[1])
    gram = packed * scale * scale
    eye = jnp.where((lane == row) | (lane == row + side), 3.4445, 0.0)
    total = None
    for step in range(ITERS):
        factor = eye + (-4.775 * gram + 2.0315 * times(gram, right(gram, side)))
        factors = right(factor, side)
        if step == ITERS - 1:
            total = times(total, factors)
        elif total is None:
            total = factor
            gram = times(times(gram, factors), factors)
        else:
            pair = times(jnp.concatenate([gram, total], axis=0), factors)
            gram, total = times(pair[:side], factors), pair[side:]
    return total * scale


def kernel(
    cols, grad, moment, back, mom, old, mid, held, made, omid, xs, obuf, mine, theirs, fac,
    load_sem, in1_r, in2_r, o1_r, end_r, rs_r, ag_r, sent,
):
    me, col = lax.axis_index("rows"), lax.axis_index("cols")
    z, y = me // RING, lax.rem(me, RING)
    mats, share, width = mom.shape[2:]
    side = RING * RING * share
    count = mats // CHUNKS
    half = count // 2
    pairs = count // 2
    workers = cols // pairs
    others = range(1, RING)
    order = (1, 3, 2)
    after = pl.ds(1, RING - 1)

    def up(at, k):
        return lax.rem(at + k, RING)

    def down(at, k):
        return lax.rem(at + RING - k, RING)

    def along(h, at):
        return (z * RING + at, col) if h == 0 else (at * RING + y, col)

    def col_peer(k):
        return lax.rem(col + k, cols)

    def all_of(ref, sem):
        pltpu.make_async_copy(ref, ref, sem).wait()

    def remote(src, dst, send, recv, to):
        return pltpu.make_async_remote_copy(
            src_ref=src, dst_ref=dst, send_sem=send, recv_sem=recv,
            device_id=to, device_id_type=MESH,
        )

    barrier = pltpu.get_barrier_semaphore()
    for k in others:
        for h in (0, 1):
            pl.semaphore_signal(
                barrier, inc=1, device_id=along(h, up((y, z)[h], k)), device_id_type=MESH
            )
    for k in range(1, cols):
        pl.semaphore_signal(barrier, inc=1, device_id=(me, col_peer(k)), device_id_type=MESH)

    def load(c):
        at = pl.ds(c * count, count)
        return [
            pltpu.make_async_copy(src.at[:, :, at], dst.at[:, :, at], load_sem.at[n, c])
            for n, (src, dst) in enumerate(((grad, mom), (moment, old)))
        ]

    for c in range(CHUNKS):
        for copy in load(c):
            copy.start()

    def meet(_):
        pl.semaphore_wait(barrier, 2 * (RING - 1) + cols - 1)

    def momentum_stage(c):
        for copy in load(c):
            copy.wait()

        @pl.loop(0, RING * RING)
        def _(i):
            at = (i // RING, lax.rem(i, RING), pl.ds(c * count, count))
            mom[at] = hold_rate * old[at] + mom[at]

    def of(h, c):
        return pl.ds(c * count + h * half, half), pl.ds(c * half, half)

    def in1(c, h, k):
        at, near = of(h, c)
        to = up((y, z)[h], k)
        src = mom.at[:, to, at] if h == 0 else mom.at[to, :, at]
        return remote(src, mid.at[h, k, :, near], sent.at[0], in1_r.at[c], along(h, to))

    def in2(c, h, k):
        at, near = of(h, c)
        to = up((z, y)[h], k)
        dst = held.at[k, after, at] if h == 0 else held.at[after, k, at]
        return remote(mid.at[h, after, to, near], dst, sent.at[1], in2_r.at[c], along(1 - h, to))

    def in3(c, h, k):
        at, _ = of(h, c)
        to = up((z, y)[h], k)
        src, dst = (
            (mom.at[to, y, at], held.at[k, 0, at]) if h == 0
            else (mom.at[z, to, at], held.at[0, k, at])
        )
        return remote(src, dst, sent.at[2], in2_r.at[c], along(1 - h, to))

    def out1(c, h, k):
        at, near = of(h, c)
        to = down((z, y)[h], k)
        src, dst = (
            (made.at[k, after, at], omid.at[0, after, z, near]) if h == 0
            else (made.at[after, k, at], omid.at[1, after, y, near])
        )
        return remote(src, dst, sent.at[3], o1_r.at[c], along(1 - h, to))

    def out3(c, h, k):
        at, _ = of(h, c)
        to = down((z, y)[h], k)
        src = made.at[k, 0, at] if h == 0 else made.at[0, k, at]
        return remote(src, back.at[z, y, at], sent.at[4], end_r.at[0], along(1 - h, to))

    def out2(c, h, k):
        at, near = of(h, c)
        to = down((y, z)[h], k)
        dst = back.at[:, y, at] if h == 0 else back.at[z, :, at]
        return remote(omid.at[h, k, :, near], dst, sent.at[5], end_r.at[1], along(h, to))

    def out(c, dz, dy):
        at = pl.ds(c * count, count)
        n = 0 if dz == 0 else 1
        return remote(
            made.at[dz, dy, at], back.at[z, y, at], sent.at[3 + n], end_r.at[n],
            (down(z, dz) * RING + down(y, dy), col),
        )

    def worker(c, p):
        return workers * p + c % workers

    def gram_send(c, p):
        to = worker(c, p)
        k = lax.rem(col + cols - to, cols)
        return remote(mine.at[c, p], theirs.at[c, k], sent.at[6], rs_r.at[c], (me, to))

    def fac_send(c, p, k):
        return remote(fac.at[c, p], fac.at[c, p], sent.at[7], ag_r.at[c], (me, col_peer(k)))

    def start_in1(c):
        for k in order:
            for h in (0, 1):
                in1(c, h, k).start()

    def rows_of(h, i, m, near):
        dz, dy = i // RING, i % RING
        if i == 0:
            return mom[z, y, m]
        if h == 0 and dz == 0:
            return mid[0, dy, z, near]
        if h == 1 and dy == 0:
            return mid[1, dz, y, near]
        return held[dz, dy, m]

    def keep_rows(h, i, m, near, value):
        dz, dy = i // RING, i % RING
        if i == 0:
            back[z, y, m] = value
        elif OUT_HOPS == 2 and h == 0 and dz == 0:
            omid[0, dy, z, near] = value
        elif OUT_HOPS == 2 and h == 1 and dy == 0:
            omid[1, dz, y, near] = value
        else:
            made[dz, dy, m] = value

    def gram_stage(c):
        all_of(held.at[after, :, pl.ds(c * count, count)], in2_r.at[c])
        first = lax.broadcasted_iota(jnp.int32, (side, 2 * side), 1) < side

        @pl.loop(0, pairs // 2)
        def _(q):
            for h in (0, 1):
                p = h * (pairs // 2) + q
                for at in (0, 1):
                    near = c * half + 2 * q + at
                    m = c * count + h * half + 2 * q + at
                    for i in range(RING * RING):
                        xs[c, p, pl.ds(at * side + i * share, share), :] = rows_of(h, i, m, near)
            for h in (0, 1):
                p = h * (pairs // 2) + q
                x = xs[c, p]
                both = mul_t(x, x)
                mine[c, p] = jnp.where(first, both[:side], both[side:])

        for p in range(pairs):
            @pl.when(worker(c, p) != col)
            def _():
                gram_send(c, p).start()

    def works(c):
        return lax.rem(col, workers) == c % workers

    def transform_stage(c):
        @pl.when(works(c))
        def _():
            place = col // workers
            all_of(theirs.at[c, pl.ds(1, cols - 1)], rs_r.at[c])
            one = mine[c, place]
            for k in range(1, cols):
                one = one + theirs[c, k]
            fac[c, place] = transform(one, side)
            for k in range(1, cols):
                fac_send(c, place, k).start()

    def apply_stage(c):
        @pl.when(works(c))
        def _():
            all_of(fac.at[c, pl.ds(0, pairs - 1)], ag_r.at[c])

        @pl.when(jnp.logical_not(works(c)))
        def _():
            all_of(fac.at[c], ag_r.at[c])

        @pl.loop(0, pairs // 2)
        def _(q):
            for h in (0, 1):
                p = h * (pairs // 2) + q
                obuf[h] = mul(spread(fac[c, p], side), xs[c, p])
            for h in (0, 1):
                for at in (0, 1):
                    near = c * half + 2 * q + at
                    m = c * count + h * half + 2 * q + at
                    for i in range(RING * RING):
                        keep_rows(h, i, m, near, obuf[h, pl.ds(at * side + i * share, share), :])

        if OUT_HOPS == 2:
            for k in order:
                for h in (0, 1):
                    out1(c, h, k).start()
                    out3(c, h, k).start()
        else:
            for dz, dy in FAR:
                out(c, dz, dy).start()

    def forward_in(c):
        all_of(mid.at[:, after, :, pl.ds(c * half, half)], in1_r.at[c])
        for k in order:
            for h in (0, 1):
                in2(c, h, k).start()
                in3(c, h, k).start()

    def forward_out(c):
        if OUT_HOPS == 2:
            all_of(omid.at[:, after, after, pl.ds(c * half, half)], o1_r.at[c])
            for k in order:
                for h in (0, 1):
                    out2(c, h, k).start()

    stages = {
        "M": momentum_stage, "B": meet, "S": start_in1, "I": forward_in, "G": gram_stage,
        "T": transform_stage, "A": apply_stage, "O": forward_out,
    }
    for event in SCHEDULE:
        stages[event[0]](int(event[1:]))

    if OUT_HOPS == 2:
        all_of(back.at[0, after], end_r.at[0])
        all_of(back.at[after], end_r.at[1])
        all_of(made.at[after, after], sent.at[3])
        all_of(made.at[0, after], sent.at[4])
        all_of(made.at[after], sent.at[5])
    else:
        all_of(back.at[0, after], end_r.at[0])
        all_of(back.at[after], end_r.at[1])
        all_of(made.at[0, after], sent.at[3])
        all_of(made.at[after], sent.at[4])
    all_of(mom.at[after], sent.at[0])
    all_of(mom.at[after, after], sent.at[1])
    all_of(mom.at[0, after], sent.at[2])
    all_of(theirs.at[pl.ds(0, 2), pl.ds(1, cols - 1)], sent.at[6])
    all_of(theirs.at[pl.ds(0, 2), pl.ds(1, cols - 1)], sent.at[7])


FAR = [(2, 2), (2, 3), (3, 2), (2, 1), (1, 2), (2, 0), (0, 2), (3, 1), (1, 3), (3, 3), (1, 1), (3, 0), (0, 3), (1, 0), (0, 1)]


def exchange_and_iterate(grad, moment, cols):
    every, share, width = grad.shape
    mats = every // (RING * RING)
    side = RING * RING * share
    count = mats // CHUNKS
    pairs = count // 2
    f32, dma = jnp.float32, pltpu.SemaphoreType.DMA
    shape = (RING, RING, mats, share, width)
    halves = (2, RING, RING, mats // 2, share, width)
    whole = pl.BlockSpec(memory_space=pltpu.VMEM)
    back, mom = pl.pallas_call(
        functools.partial(kernel, cols),
        out_shape=[jax.ShapeDtypeStruct(shape, f32)] * 2,
        in_specs=[pl.BlockSpec(memory_space=pltpu.HBM)] * 2,
        out_specs=[whole, whole],
        scratch_shapes=[
            pltpu.VMEM(shape, f32),
            pltpu.VMEM(halves, f32),
            pltpu.VMEM(shape, f32),
            pltpu.VMEM(shape, f32),
            pltpu.VMEM(halves, f32),
            pltpu.VMEM((CHUNKS, pairs, 2 * side, width), f32),
            pltpu.VMEM((2, 2 * side, width), f32),
            pltpu.VMEM((CHUNKS, pairs, side, 2 * side), f32),
            pltpu.VMEM((CHUNKS, cols, side, 2 * side), f32),
            pltpu.VMEM((CHUNKS, pairs, side, 2 * side), f32),
            dma((2, CHUNKS)), dma((CHUNKS,)), dma((CHUNKS,)), dma((CHUNKS,)), dma((2,)),
            dma((CHUNKS,)), dma((CHUNKS,)), dma((8,)),
        ],
        compiler_params=pltpu.CompilerParams(
            collective_id=0, has_side_effects=True, vmem_limit_bytes=40 * 2**20
        ),
        name="exchange_and_iterate",
    )(*(pltpu.with_memory_space_constraint(v.reshape(shape), pltpu.HBM) for v in (grad, moment)))
    return back.reshape(grad.shape), mom.reshape(grad.shape)


def solution(mesh):
    cols = mesh.shape["cols"]

    def on_device(grad_stack, moment_stack, weight_stack):
        back, new_momentum = exchange_and_iterate(grad_stack, moment_stack, cols)
        new_weights = weight_stack - learn_rate * back
        return (new_weights, new_momentum)

    placed = P(None, "rows", "cols")
    return jax.shard_map(
        on_device,
        mesh=mesh,
        in_specs=(placed, placed, placed),
        out_specs=(placed, placed),
        check_vma=False,
    )
```

time: 78.1 us -> 62.4 us (0.80); the launches traced: 78 us -> 61.3 us
  Pallas kernels: 72.4 us -> 57.3 us
  other arithmetic: 4.94 us -> 2 us
  local copies, waits for them, and re-layouts: 0.01 us -> 1.32 us
    pallas_call x1, Pallas kernels: 72.4 us -> 57.3 us  [exchange_and_iterate(): pl.pallas_call(functools.partial(kernel, cols), out_shape=[jax.ShapeDtype...]
    add x1 -> x0, other arithmetic: 2.94 us -> none  [on_device(): new_momentum = hold_rate * moment_stack + grad_stack]
    unnamed x4 -> x3, local copies, waits for them, and re-layouts: 0.01 us -> 1.32 us
where the time goes in v2:
time: 62.4 us; the launch traced here: 61.3 us
  Pallas kernels  57.3 us (92%)
  other arithmetic  2 us (3%)
  local copies, waits for them, and re-layouts  1.32 us (2%)
  between operations  0.65 us (1%)
    pallas_call x1, Pallas kernels, exchange_and_iterate(): pl.pallas_call(functools.partial(kernel, cols), out_shape=[jax.ShapeDtype...  57.3 us
    sub x1, other arithmetic, on_device(): new_weights = weight_stack - learn_rate * back  2 us
    unnamed x3, local copies, waits for them, and re-layouts  1.32 us

profile of v2, /device:TPU:0, one launch (start us, length us, event | category | flops | bytes accessed | tf_op | source)
XLA Modules:
  0.0 61.3 jit_solution(1443972116387920997)
XLA Ops:
  0.6 0.0 copy-start
  0.6 57.3 %exchange_and_iterate.1 = (f32[4,4,32,4,256]{4,3,2,1,0:T(4,128)S(1)}, f32[4,4,32,4,256]{4,3,2,1,0:T(4,128)S(1)}) custom-call(f32[4,4,32,4,256]{4,3,2,1,0:T(4,128)} %bitcast.6, f32[4,4,32,4,256]{4,3,2,1,0:T(4,128)} %bitcast.7), custom_call_target="tpu_custom_call" | custom-call | tf_op jit(solution)/shard_map/exchange_and_iterate/pallas_call | solution.py:392
  58.0 0.0 copy-done
  58.0 2.0 %bitcast_subtract_fusion = f32[512,4,256]{2,1,0:T(4,128)} fusion(f32[512,4,256]{2,1,0:T(4,128)S(1)} %copy-done, f32[4,4,32,4,256]{4,3,2,1,0:T(4,128)S(1)} %get-tuple-element.4), kind=kLoop, calls=%fused_computation | loop fusion | flops 524288 | bytes 6291456 | tf_op jit(solution)/shard_map/sub | solution.py:424
  60.0 1.3 %copy.6 = f32[512,4,256]{2,1,0:T(4,128)} copy(f32[512,4,256]{2,1,0:T(4,128)S(1)} %bitcast.5) | data formatting | bytes 4194304
Async XLA Ops:
  0.6 57.3 %copy-start = (f32[512,4,256]{2,1,0:T(4,128)S(1)}, f32[512,4,256]{2,1,0:T(4,128)}, u32[]{:S(2)}) copy-start(f32[512,4,256]{2,1,0:T(4,128)} %param.5) | copy-start | bytes 6291460

commit v3 on v2

--- a/solution.py
+++ b/solution.py
@@ -12,11 +12,11 @@
 CHUNKS = 8
 OUT_HOPS = 2
 SCHEDULE = (
-    "M0", "M4", "B0", "S4", "M2", "M1", "M5", "M3", "S3", "S1", "S2", "I4", "I3", "I1",
-    "I2", "S5", "S0", "G4", "G3", "M6", "M7", "S6", "S7", "G1", "G2", "I5", "T4", "I0",
-    "T3", "I6", "T1", "I7", "T2", "A4", "G5", "A3", "G0", "G6", "A1", "G7", "A2", "O4",
-    "T5", "O3", "T6", "T0", "O1", "T7", "O2", "A5", "A0", "A6", "A7", "O5", "O0", "O6",
-    "O7",
+    "M1", "B0", "S1", "M5", "M0", "M7", "M4", "S0", "S7", "S5", "I1", "M6", "I0", "I7",
+    "I5", "G1", "M2", "S2", "G0", "S4", "M3", "S6", "S3", "G7", "G5", "I2", "T1", "T0",
+    "I4", "T7", "I6", "T5", "I3", "A1", "G2", "A0", "G4", "A7", "G6", "G3", "A5", "O1",
+    "T2", "O0", "T4", "O7", "T3", "T6", "O5", "A2", "A4", "A6", "A3", "O2", "O4", "O6",
+    "O3",
 )
 
 hold_rate = 0.95
@@ -416,13 +416,53 @@
     return back.reshape(grad.shape), mom.reshape(grad.shape)
 
 
+FINAL = 8
+
+
+def finish_kernel(weight, back, mom, new_weight, new_mom, made, sems):
+    step = weight.shape[0] // FINAL
+    whole = pltpu.make_async_copy(mom, new_mom, sems.at[FINAL])
+    whole.start()
+
+    def put(i):
+        at = pl.ds(i * step, step)
+        return pltpu.make_async_copy(made.at[at], new_weight.at[at], sems.at[i])
+
+    @pl.loop(0, FINAL)
+    def _(i):
+        at = pl.ds(i * step, step)
+        made[at] = weight[at] - learn_rate * back[at]
+        put(i).start()
+
+    @pl.loop(0, FINAL)
+    def _(i):
+        put(i).wait()
+    whole.wait()
+
+
+def finish(weight, back, mom):
+    here = pl.BlockSpec(memory_space=pltpu.VMEM)
+    out = pl.BlockSpec(memory_space=pl.ANY)
+    shape = jax.ShapeDtypeStruct(weight.shape, jnp.float32)
+    return pl.pallas_call(
+        finish_kernel,
+        out_shape=[shape, shape],
+        in_specs=[here] * 3,
+        out_specs=[out, out],
+        scratch_shapes=[
+            pltpu.VMEM(weight.shape, jnp.float32), pltpu.SemaphoreType.DMA((FINAL + 1,)),
+        ],
+        compiler_params=pltpu.CompilerParams(vmem_limit_bytes=16 * 2**20),
+        name="finish",
+    )(weight, back, mom)
+
+
 def solution(mesh):
     cols = mesh.shape["cols"]
 
     def on_device(grad_stack, moment_stack, weight_stack):
         back, new_momentum = exchange_and_iterate(grad_stack, moment_stack, cols)
-        new_weights = weight_stack - learn_rate * back
-        return (new_weights, new_momentum)
+        return tuple(finish(weight_stack, back, new_momentum))
 
     placed = P(None, "rows", "cols")
     return jax.shard_map(

time: 62.4 us -> 59.1 us (0.947)
  other arithmetic: 2 us -> 0 us
  local copies, waits for them, and re-layouts: 1.32 us -> 0.01 us
    pallas_call x0 -> x1, Pallas kernels: none -> 2.08 us  [finish(): pl.pallas_call(finish_kernel, out_shape=[shape, shape], in_specs=[here] *...]
    sub x1 -> x0, other arithmetic: 2 us -> none  [on_device(): new_weights = weight_stack - learn_rate * back]
    pallas_call x1, Pallas kernels: 57.3 us -> 55.6 us  [exchange_and_iterate(): pl.pallas_call(functools.partial(kernel, cols), out_shape=[jax.ShapeDtype...]
    unnamed x3 -> x2, local copies, waits for them, and re-layouts: 1.32 us -> 0.01 us
where the time goes in v3:
time: 59.1 us; the launch traced here: 58.3 us
  Pallas kernels  57.6 us (97%)
  between operations  0.65 us (1%)
    pallas_call x1, Pallas kernels, exchange_and_iterate(): pl.pallas_call(functools.partial(kernel, cols), out_shape=[jax.ShapeDtype...  55.6 us
    pallas_call x1, Pallas kernels, finish(): pl.pallas_call(finish_kernel, out_shape=[shape, shape], in_specs=[here] *...  2.08 us

profile of v3, /device:TPU:0, one launch (start us, length us, event | category | flops | bytes accessed | tf_op | source)
XLA Modules:
  0.0 58.3 jit_solution(17064840849492002351)
XLA Ops:
  0.6 0.0 copy-start
  0.6 55.6 %exchange_and_iterate.1 = (f32[4,4,32,4,256]{4,3,2,1,0:T(4,128)S(1)}, f32[4,4,32,4,256]{4,3,2,1,0:T(4,128)S(1)}) custom-call(f32[4,4,32,4,256]{4,3,2,1,0:T(4,128)} %bitcast.6, f32[4,4,32,4,256]{4,3,2,1,0:T(4,128)} %bitcast.7), custom_call_target="tpu_custom_call" | custom-call | tf_op jit(solution)/shard_map/exchange_and_iterate/pallas_call | solution.py:392
  56.2 0.0 copy-done
  56.2 2.1 %finish.1 = (f32[512,4,256]{2,1,0:T(4,128)}, f32[512,4,256]{2,1,0:T(4,128)}) custom-call(f32[512,4,256]{2,1,0:T(4,128)S(1)} %copy-done, f32[512,4,256]{2,1,0:T(4,128)S(1)} %bitcast.4, f32[512,4,256]{2,1,0:T(4,128)S(1)} %bitcast.5), custom_call_target="tpu_custom_call" | custom-call | tf_op jit(solution)/shard_map/finish/pallas_call | solution.py:447
Async XLA Ops:
  0.6 55.6 %copy-start = (f32[512,4,256]{2,1,0:T(4,128)S(1)}, f32[512,4,256]{2,1,0:T(4,128)}, u32[]{:S(2)}) copy-start(f32[512,4,256]{2,1,0:T(4,128)} %weight.1) | copy-start | bytes 6291460

commit v4 on v3

--- a/solution.py
+++ b/solution.py
@@ -10,7 +10,6 @@
 ITERS = 5
 RING = 4
 CHUNKS = 8
-OUT_HOPS = 2
 SCHEDULE = (
     "M1", "B0", "S1", "M5", "M0", "M7", "M4", "S0", "S7", "S5", "I1", "M6", "I0", "I7",
     "I5", "G1", "M2", "S2", "G0", "S4", "M3", "S6", "S3", "G7", "G5", "I2", "T1", "T0",
@@ -42,7 +41,10 @@
 def spread(packed, side):
     first = lax.broadcasted_iota(jnp.int32, (side, 2 * side), 1) < side
     return jnp.concatenate(
-        [jnp.where(first, packed, 0.0), jnp.where(first, 0.0, packed)], axis=0
+        [
+            jnp.where(first, packed, jnp.zeros_like(packed)),
+            jnp.where(first, jnp.zeros_like(packed), packed),
+        ], axis=0,
     )
 
 
@@ -55,9 +57,7 @@
 
 
 def right(x, side):
-    high, mid, low = (part.astype(jnp.bfloat16) for part in map(
-        lambda part: spread(part.astype(jnp.float32), side), parts(x)
-    ))
+    high, mid, low = (spread(part, side) for part in parts(x))
     both = jnp.concatenate(
         [jnp.concatenate([high, mid], axis=1), jnp.concatenate([mid, high], axis=1)], axis=0
     )
@@ -96,16 +96,18 @@
     eye = jnp.where((lane == row) | (lane == row + side), 3.4445, 0.0)
     total = None
     for step in range(ITERS):
-        factor = eye + (-4.775 * gram + 2.0315 * times(gram, right(gram, side)))
+        grams = right(gram, side)
+        factor = eye + (-4.775 * gram + 2.0315 * times(gram, grams))
+        if step == ITERS - 1:
+            total = times(factor, right(total, side))
+            break
+        inner = times(factor, grams)
         factors = right(factor, side)
-        if step == ITERS - 1:
-            total = times(total, factors)
-        elif total is None:
-            total = factor
-            gram = times(times(gram, factors), factors)
+        if total is None:
+            gram, total = times(inner, factors), factor
         else:
-            pair = times(jnp.concatenate([gram, total], axis=0), factors)
-            gram, total = times(pair[:side], factors), pair[side:]
+            pair = times(jnp.concatenate([inner, total], axis=0), factors)
+            gram, total = pair[:side], pair[side:]
     return total * scale
 
 
@@ -122,7 +124,7 @@
     pairs = count // 2
     workers = cols // pairs
     others = range(1, RING)
-    order = (1, 3, 2)
+    order = (2, 1, 3)
     after = pl.ds(1, RING - 1)
 
     def up(at, k):
@@ -162,24 +164,36 @@
             for n, (src, dst) in enumerate(((grad, mom), (moment, old)))
         ]
 
-    for c in range(CHUNKS):
-        for copy in load(c):
-            copy.start()
+    loads = [int(event[1:]) for event in SCHEDULE if event[0] == "M"]
+
+    def start_loads(some):
+        for c in some:
+            for copy in load(c):
+                copy.start()
+
+    start_loads(loads[:2])
 
     def meet(_):
         pl.semaphore_wait(barrier, 2 * (RING - 1) + cols - 1)
+
+    def of(h, c):
+        return pl.ds(c * count + h * half, half), pl.ds(c * half, half)
 
     def momentum_stage(c):
         for copy in load(c):
             copy.wait()
+        if c == loads[0]:
+            start_loads(loads[2:])
 
         @pl.loop(0, RING * RING)
         def _(i):
             at = (i // RING, lax.rem(i, RING), pl.ds(c * count, count))
             mom[at] = hold_rate * old[at] + mom[at]
 
-    def of(h, c):
-        return pl.ds(c * count + h * half, half), pl.ds(c * half, half)
+        for h in (0, 1):
+            at, near = of(h, c)
+            for k in range(RING):
+                mid[h, 0, k, near] = mom[k, y, at] if h == 0 else mom[z, k, at]
 
     def in1(c, h, k):
         at, near = of(h, c)
@@ -190,46 +204,23 @@
     def in2(c, h, k):
         at, near = of(h, c)
         to = up((z, y)[h], k)
-        dst = held.at[k, after, at] if h == 0 else held.at[after, k, at]
-        return remote(mid.at[h, after, to, near], dst, sent.at[1], in2_r.at[c], along(1 - h, to))
-
-    def in3(c, h, k):
-        at, _ = of(h, c)
-        to = up((z, y)[h], k)
-        src, dst = (
-            (mom.at[to, y, at], held.at[k, 0, at]) if h == 0
-            else (mom.at[z, to, at], held.at[0, k, at])
-        )
-        return remote(src, dst, sent.at[2], in2_r.at[c], along(1 - h, to))
+        dst = held.at[k, :, at] if h == 0 else held.at[:, k, at]
+        return remote(mid.at[h, :, to, near], dst, sent.at[1], in2_r.at[c], along(1 - h, to))
 
     def out1(c, h, k):
         at, near = of(h, c)
         to = down((z, y)[h], k)
         src, dst = (
-            (made.at[k, after, at], omid.at[0, after, z, near]) if h == 0
-            else (made.at[after, k, at], omid.at[1, after, y, near])
+            (made.at[k, :, at], omid.at[0, :, z, near]) if h == 0
+            else (made.at[:, k, at], omid.at[1, :, y, near])
         )
-        return remote(src, dst, sent.at[3], o1_r.at[c], along(1 - h, to))
-
-    def out3(c, h, k):
-        at, _ = of(h, c)
-        to = down((z, y)[h], k)
-        src = made.at[k, 0, at] if h == 0 else made.at[0, k, at]
-        return remote(src, back.at[z, y, at], sent.at[4], end_r.at[0], along(1 - h, to))
+        return remote(src, dst, sent.at[2], o1_r.at[c], along(1 - h, to))
 
     def out2(c, h, k):
         at, near = of(h, c)
         to = down((y, z)[h], k)
         dst = back.at[:, y, at] if h == 0 else back.at[z, :, at]
-        return remote(omid.at[h, k, :, near], dst, sent.at[5], end_r.at[1], along(h, to))
-
-    def out(c, dz, dy):
-        at = pl.ds(c * count, count)
-        n = 0 if dz == 0 else 1
-        return remote(
-            made.at[dz, dy, at], back.at[z, y, at], sent.at[3 + n], end_r.at[n],
-            (down(z, dz) * RING + down(y, dy), col),
-        )
+        return remote(omid.at[h, k, :, near], dst, sent.at[3], end_r, along(h, to))
 
     def worker(c, p):
         return workers * p + c % workers
@@ -237,10 +228,10 @@
     def gram_send(c, p):
         to = worker(c, p)
         k = lax.rem(col + cols - to, cols)
-        return remote(mine.at[c, p], theirs.at[c, k], sent.at[6], rs_r.at[c], (me, to))
+        return remote(mine.at[c, p], theirs.at[c, k], sent.at[4], rs_r.at[c], (me, to))
 
     def fac_send(c, p, k):
-        return remote(fac.at[c, p], fac.at[c, p], sent.at[7], ag_r.at[c], (me, col_peer(k)))
+        return remote(fac.at[c, p], fac.at[c, p], sent.at[5], ag_r.at[c], (me, col_peer(k)))
 
     def start_in1(c):
         for k in order:
@@ -261,9 +252,9 @@
         dz, dy = i // RING, i % RING
         if i == 0:
             back[z, y, m] = value
-        elif OUT_HOPS == 2 and h == 0 and dz == 0:
+        elif h == 0 and dz == 0:
             omid[0, dy, z, near] = value
-        elif OUT_HOPS == 2 and h == 1 and dy == 0:
+        elif h == 1 and dy == 0:
             omid[1, dz, y, near] = value
         else:
             made[dz, dy, m] = value
@@ -328,28 +319,29 @@
                     for i in range(RING * RING):
                         keep_rows(h, i, m, near, obuf[h, pl.ds(at * side + i * share, share), :])
 
-        if OUT_HOPS == 2:
-            for k in order:
-                for h in (0, 1):
-                    out1(c, h, k).start()
-                    out3(c, h, k).start()
-        else:
-            for dz, dy in FAR:
-                out(c, dz, dy).start()
+        for k in order:
+            for h in (0, 1):
+                out1(c, h, k).start()
 
     def forward_in(c):
         all_of(mid.at[:, after, :, pl.ds(c * half, half)], in1_r.at[c])
         for k in order:
             for h in (0, 1):
                 in2(c, h, k).start()
-                in3(c, h, k).start()
 
     def forward_out(c):
-        if OUT_HOPS == 2:
-            all_of(omid.at[:, after, after, pl.ds(c * half, half)], o1_r.at[c])
-            for k in order:
-                for h in (0, 1):
-                    out2(c, h, k).start()
+        all_of(omid.at[:, :, after, pl.ds(c * half, half)], o1_r.at[c])
+        for k in order:
+            for h in (0, 1):
+                out2(c, h, k).start()
+        for h in (0, 1):
+            at, near = of(h, c)
+            for k in others:
+                here = up((z, y)[h], k)
+                if h == 0:
+                    back[here, y, at] = omid[0, 0, here, near]
+                else:
+                    back[z, here, at] = omid[1, 0, here, near]
 
     stages = {
         "M": momentum_stage, "B": meet, "S": start_in1, "I": forward_in, "G": gram_stage,
@@ -358,25 +350,13 @@
     for event in SCHEDULE:
         stages[event[0]](int(event[1:]))
 
-    if OUT_HOPS == 2:
-        all_of(back.at[0, after], end_r.at[0])
-        all_of(back.at[after], end_r.at[1])
-        all_of(made.at[after, after], sent.at[3])
-        all_of(made.at[0, after], sent.at[4])
-        all_of(made.at[after], sent.at[5])
-    else:
-        all_of(back.at[0, after], end_r.at[0])
-        all_of(back.at[after], end_r.at[1])
-        all_of(made.at[0, after], sent.at[3])
-        all_of(made.at[after], sent.at[4])
+    all_of(back.at[after], end_r)
     all_of(mom.at[after], sent.at[0])
-    all_of(mom.at[after, after], sent.at[1])
-    all_of(mom.at[0, after], sent.at[2])
-    all_of(theirs.at[pl.ds(0, 2), pl.ds(1, cols - 1)], sent.at[6])
-    all_of(theirs.at[pl.ds(0, 2), pl.ds(1, cols - 1)], sent.at[7])
-
-
-FAR = [(2, 2), (2, 3), (3, 2), (2, 1), (1, 2), (2, 0), (0, 2), (3, 1), (1, 3), (3, 3), (1, 1), (3, 0), (0, 3), (1, 0), (0, 1)]
+    all_of(mom.at[after], sent.at[1])
+    all_of(made.at[after], sent.at[2])
+    all_of(made.at[after], sent.at[3])
+    all_of(theirs.at[pl.ds(0, 2), pl.ds(1, cols - 1)], sent.at[4])
+    all_of(theirs.at[pl.ds(0, 2), pl.ds(1, cols - 1)], sent.at[5])
 
 
 def exchange_and_iterate(grad, moment, cols):
@@ -405,8 +385,8 @@
             pltpu.VMEM((CHUNKS, pairs, side, 2 * side), f32),
             pltpu.VMEM((CHUNKS, cols, side, 2 * side), f32),
             pltpu.VMEM((CHUNKS, pairs, side, 2 * side), f32),
-            dma((2, CHUNKS)), dma((CHUNKS,)), dma((CHUNKS,)), dma((CHUNKS,)), dma((2,)),
-            dma((CHUNKS,)), dma((CHUNKS,)), dma((8,)),
+            dma((2, CHUNKS)), dma((CHUNKS,)), dma((CHUNKS,)), dma((CHUNKS,)), dma(()),
+            dma((CHUNKS,)), dma((CHUNKS,)), dma((6,)),
         ],
         compiler_params=pltpu.CompilerParams(
             collective_id=0, has_side_effects=True, vmem_limit_bytes=40 * 2**20

time: 59.1 us -> 59 us (level)
  no operation moved by 1% of the time
where the time goes in v4:
time: 59 us; the launch traced here: 58 us
  Pallas kernels  57.4 us (97%)
  between operations  0.65 us (1%)
    pallas_call x1, Pallas kernels, exchange_and_iterate(): pl.pallas_call(functools.partial(kernel, cols), out_shape=[jax.ShapeDtype...  55.3 us
    pallas_call x1, Pallas kernels, finish(): pl.pallas_call(finish_kernel, out_shape=[shape, shape], in_specs=[here] *...  2.08 us

profile of v4, /device:TPU:0, one launch (start us, length us, event | category | flops | bytes accessed | tf_op | source)
XLA Modules:
  0.0 58.0 jit_solution(1060484669133812542)
XLA Ops:
  0.6 0.0 copy-start
  0.6 55.3 %exchange_and_iterate.1 = (f32[4,4,32,4,256]{4,3,2,1,0:T(4,128)S(1)}, f32[4,4,32,4,256]{4,3,2,1,0:T(4,128)S(1)}) custom-call(f32[4,4,32,4,256]{4,3,2,1,0:T(4,128)} %bitcast.6, f32[4,4,32,4,256]{4,3,2,1,0:T(4,128)} %bitcast.7), custom_call_target="tpu_custom_call" | custom-call | tf_op jit(solution)/shard_map/exchange_and_iterate/pallas_call | solution.py:372
  55.9 0.0 copy-done
  55.9 2.1 %finish.1 = (f32[512,4,256]{2,1,0:T(4,128)}, f32[512,4,256]{2,1,0:T(4,128)}) custom-call(f32[512,4,256]{2,1,0:T(4,128)S(1)} %copy-done, f32[512,4,256]{2,1,0:T(4,128)S(1)} %bitcast.4, f32[512,4,256]{2,1,0:T(4,128)S(1)} %bitcast.5), custom_call_target="tpu_custom_call" | custom-call | tf_op jit(solution)/shard_map/finish/pallas_call | solution.py:427
Async XLA Ops:
  0.6 55.3 %copy-start = (f32[512,4,256]{2,1,0:T(4,128)S(1)}, f32[512,4,256]{2,1,0:T(4,128)}, u32[]{:S(2)}) copy-start(f32[512,4,256]{2,1,0:T(4,128)} %weight.1) | copy-start | bytes 6291460

commit v5 on v4

--- a/solution.py
+++ b/solution.py
@@ -223,7 +223,7 @@
         return remote(omid.at[h, k, :, near], dst, sent.at[3], end_r, along(h, to))
 
     def worker(c, p):
-        return workers * p + c % workers
+        return workers * p + (c + 1) % workers
 
     def gram_send(c, p):
         to = worker(c, p)
@@ -284,7 +284,7 @@
                 gram_send(c, p).start()
 
     def works(c):
-        return lax.rem(col, workers) == c % workers
+        return lax.rem(col, workers) == (c + 1) % workers
 
     def transform_stage(c):
         @pl.when(works(c))
@@ -396,7 +396,7 @@
     return back.reshape(grad.shape), mom.reshape(grad.shape)
 
 
-FINAL = 8
+FINAL = 4
 
 
 def finish_kernel(weight, back, mom, new_weight, new_mom, made, sems):

time: 59 us -> 58.7 us (level)
  no operation moved by 1% of the time
where the time goes in v5:
time: 58.7 us; the launch traced here: 57.6 us
  Pallas kernels  56.9 us (97%)
  between operations  0.65 us (1%)
    pallas_call x1, Pallas kernels, exchange_and_iterate(): pl.pallas_call(functools.partial(kernel, cols), out_shape=[jax.ShapeDtype...  54.9 us
    pallas_call x1, Pallas kernels, finish(): pl.pallas_call(finish_kernel, out_shape=[shape, shape], in_specs=[here] *...  2.05 us

profile of v5, /device:TPU:0, one launch (start us, length us, event | category | flops | bytes accessed | tf_op | source)
XLA Modules:
  0.0 57.6 jit_solution(15093512502113784701)
XLA Ops:
  0.6 0.0 copy-start
  0.6 54.9 %exchange_and_iterate.1 = (f32[4,4,32,4,256]{4,3,2,1,0:T(4,128)S(1)}, f32[4,4,32,4,256]{4,3,2,1,0:T(4,128)S(1)}) custom-call(f32[4,4,32,4,256]{4,3,2,1,0:T(4,128)} %bitcast.6, f32[4,4,32,4,256]{4,3,2,1,0:T(4,128)} %bitcast.7), custom_call_target="tpu_custom_call" | custom-call | tf_op jit(solution)/shard_map/exchange_and_iterate/pallas_call | solution.py:372
  55.5 0.0 copy-done
  55.6 2.0 %finish.1 = (f32[512,4,256]{2,1,0:T(4,128)}, f32[512,4,256]{2,1,0:T(4,128)}) custom-call(f32[512,4,256]{2,1,0:T(4,128)S(1)} %copy-done, f32[512,4,256]{2,1,0:T(4,128)S(1)} %bitcast.4, f32[512,4,256]{2,1,0:T(4,128)S(1)} %bitcast.5), custom_call_target="tpu_custom_call" | custom-call | tf_op jit(solution)/shard_map/finish/pallas_call | solution.py:427
Async XLA Ops:
  0.6 54.9 %copy-start = (f32[512,4,256]{2,1,0:T(4,128)S(1)}, f32[512,4,256]{2,1,0:T(4,128)}, u32[]{:S(2)}) copy-start(f32[512,4,256]{2,1,0:T(4,128)} %weight.1) | copy-start | bytes 6291460

commit v6 on v5

--- a/solution.py
+++ b/solution.py
@@ -295,7 +295,7 @@
             for k in range(1, cols):
                 one = one + theirs[c, k]
             fac[c, place] = transform(one, side)
-            for k in range(1, cols):
+            for k in sorted(range(1, cols), key=lambda k: abs(k - cols // 2)):
                 fac_send(c, place, k).start()
 
     def apply_stage(c):

time: 58.7 us -> 58.5 us (level)
  no operation moved by 1% of the time
where the time goes in v6:
time: 58.5 us; the launch traced here: 57.7 us
  Pallas kernels  57.1 us (98%)
  between operations  0.65 us (1%)
    pallas_call x1, Pallas kernels, exchange_and_iterate(): pl.pallas_call(functools.partial(kernel, cols), out_shape=[jax.ShapeDtype...  55 us
    pallas_call x1, Pallas kernels, finish(): pl.pallas_call(finish_kernel, out_shape=[shape, shape], in_specs=[here] *...  2.05 us

profile of v6, /device:TPU:0, one launch (start us, length us, event | category | flops | bytes accessed | tf_op | source)
XLA Modules:
  0.0 57.7 jit_solution(3168111864592797539)
XLA Ops:
  0.6 0.0 copy-start
  0.6 55.0 %exchange_and_iterate.1 = (f32[4,4,32,4,256]{4,3,2,1,0:T(4,128)S(1)}, f32[4,4,32,4,256]{4,3,2,1,0:T(4,128)S(1)}) custom-call(f32[4,4,32,4,256]{4,3,2,1,0:T(4,128)} %bitcast.6, f32[4,4,32,4,256]{4,3,2,1,0:T(4,128)} %bitcast.7), custom_call_target="tpu_custom_call" | custom-call | tf_op jit(solution)/shard_map/exchange_and_iterate/pallas_call | solution.py:372
  55.7 0.0 copy-done
  55.7 2.0 %finish.1 = (f32[512,4,256]{2,1,0:T(4,128)}, f32[512,4,256]{2,1,0:T(4,128)}) custom-call(f32[512,4,256]{2,1,0:T(4,128)S(1)} %copy-done, f32[512,4,256]{2,1,0:T(4,128)S(1)} %bitcast.4, f32[512,4,256]{2,1,0:T(4,128)S(1)} %bitcast.5), custom_call_target="tpu_custom_call" | custom-call | tf_op jit(solution)/shard_map/finish/pallas_call | solution.py:427
Async XLA Ops:
  0.6 55.1 %copy-start = (f32[512,4,256]{2,1,0:T(4,128)S(1)}, f32[512,4,256]{2,1,0:T(4,128)}, u32[]{:S(2)}) copy-start(f32[512,4,256]{2,1,0:T(4,128)} %weight.1) | copy-start | bytes 6291460
